TPU v7x, 32 devices: a whole 2x2x4 slice. The times are simulated.
32 devices in a mesh: groups: 2 (over y), seq: 4 (over z), heads: 2 (over x), cfg: 2 (over core).
Axes of the slice: x: 2, y: 2, z: 4, core: 2. Of those that a mesh axis runs over, the one named last changes fastest.
Arguments:
- video_tokens: bfloat16 [2, 8, 1152, 1024], P('cfg', ('groups', 'seq'), 'heads'), parts along dimension 1, may hold values from -6 to 6
- text_tokens: bfloat16 [2, 8, 1152, 128], P('cfg', ('groups', 'seq'), 'heads'), parts along dimension 1, may hold values from -6 to 6
- text_length: int32 [2, 8], P('cfg', ('groups', 'seq')), parts along dimension 1, may hold values from 1 to 128
- guide_numer: int32 [8], P(('groups', 'seq')), parts along dimension 0, may hold values from 2 to 8
- guide_denom: int32 [8], P(('groups', 'seq')), parts along dimension 0, may hold values from 4 to 8
- spatial_gain: bfloat16 [1152], replicated, may hold values from 0.25 to 1.75
- spatial_qkv: bfloat16 [3, 1152, 1152], P(None, 'heads'), may hold values from -0.11785113 to 0.11785113
- spatial_out: bfloat16 [1152, 1152], P('heads'), may hold values from -0.1875 to 0.1875
- temporal_gain: bfloat16 [1152], replicated, may hold values from 0.25 to 1.75
- temporal_qkv: bfloat16 [3, 1152, 1152], P(None, 'heads'), may hold values from -0.11785113 to 0.11785113
- temporal_out: bfloat16 [1152, 1152], P('heads'), may hold values from -0.1875 to 0.1875
Outputs:
- guided: bfloat16 [8, 1152, 1024], P(('groups', 'seq'), ('heads', 'cfg')), parts along dimension 0
There are 2 independent parts, one for each index of `groups`. A program takes and returns all parts, laid end to end along the dimension named above; an argument that names none is the same for every part. Nothing has to cross between parts.
Inputs may be any that keep to these rules, and one draw needn't show every extreme that they name: `text_length`: text tokens at or beyond a frame's length are padding.
All inputs are finite; a program needn't handle non-finite values.
Results may differ from a plain program's by a relative error of at most 0.009.
Values may be sent and summed in bfloat16 or wider, within the bound.
A program may use at most 64 MiB of HBM per device.

v0:
```python
import jax
import jax.numpy as jnp
from jax import lax
from jax.sharding import PartitionSpec as P

D = 1152
HEAD_DIM = 72
epsilon = 1e-06


def from_partner(shard, axis, stride):
    return lax.ppermute(shard, axis, [(i, i ^ 1 << stride) for i in range(lax.axis_size(axis))])


def softmax_along(scores, axis):
    top_score = jnp.max(scores, axis=axis, keepdims=True)
    expons = jnp.exp(scores - top_score)
    return (expons / jnp.sum(expons, axis=axis, keepdims=True)).astype(jnp.bfloat16)


def project_piece(piece, gain_vector, weights, parts):
    gain_piece = gain_vector.astype(jnp.float32)
    weight_piece = weights[parts]
    piece_wide = piece.astype(jnp.float32)
    scaled = (piece_wide * gain_piece[None, :, None]).astype(jnp.bfloat16)
    product = jnp.einsum("kod,fdp->fkop", weight_piece, scaled, preferred_element_type=jnp.float32)
    return (product, jnp.sum(piece_wide * piece_wide, axis=1))


def add_mixed(piece, matrix):
    return jnp.einsum("oc,fcp->fop", matrix, piece, preferred_element_type=jnp.float32)


def shards(
    video_tokens,
    text_tokens,
    text_length,
    guide_numer,
    guide_denom,
    spatial_gain,
    spatial_qkv,
    spatial_out,
    temporal_gain,
    temporal_qkv,
    temporal_out,
):
    frame_count = video_tokens.shape[1]
    width = video_tokens.shape[2]
    positions = video_tokens.shape[3]
    text_count = text_tokens.shape[3]
    local_heads = width // HEAD_DIM
    frame_tokens = video_tokens[0]
    frame_text = text_tokens[0]
    video_piece = lax.all_gather(frame_tokens, "heads", axis=1, tiled=True)
    text_piece = lax.all_gather(frame_text, "heads", axis=1, tiled=True)
    video_add, video_sq = project_piece(video_piece, spatial_gain, spatial_qkv, slice(0, 3))
    text_add, text_sq = project_piece(text_piece, spatial_gain, spatial_qkv, slice(1, 3))
    mixed = (video_add * lax.rsqrt(video_sq / D + epsilon)[:, None, None, :]).astype(jnp.bfloat16)
    mixed = mixed.reshape(frame_count, 3, local_heads, HEAD_DIM, positions)
    context = (text_add * lax.rsqrt(text_sq / D + epsilon)[:, None, None, :]).astype(jnp.bfloat16)
    context = context.reshape(frame_count, 2, local_heads, HEAD_DIM, text_count)
    key_rows = jnp.concatenate([mixed[:, 1], context[:, 0]], axis=3)
    value_rows = jnp.concatenate([mixed[:, 2], context[:, 1]], axis=3)
    query_all = mixed[:, 0]
    text_valid = jnp.arange(text_count, dtype=jnp.int32)[None, :] < text_length[0][:, None]
    valid_keys = jnp.concatenate(
        [jnp.ones((frame_count, positions), dtype=bool), text_valid], axis=1
    )
    block_rows = min(512, positions)
    block_count = positions // block_rows
    frame_ids = jnp.repeat(jnp.arange(frame_count, dtype=jnp.int32), block_count)
    block_ids = jnp.tile(jnp.arange(block_count, dtype=jnp.int32), frame_count)

    def block_step(inputs):
        frame_id, block_id = inputs
        query_rows = lax.dynamic_slice_in_dim(
            query_all[frame_id], block_id * block_rows, block_rows, 2
        )
        scores = jnp.einsum(
            "hep,hek->hpk", query_rows, key_rows[frame_id], preferred_element_type=jnp.float32
        )
        scores = scores * HEAD_DIM ** (-0.5)
        scores = jnp.where(valid_keys[frame_id][None, None, :], scores, -jnp.inf)
        weights = softmax_along(scores, 2)
        result = jnp.einsum(
            "hpk,hek->hep", weights, value_rows[frame_id], preferred_element_type=jnp.float32
        )
        return result.astype(jnp.bfloat16)

    attended = lax.map(block_step, (frame_ids, block_ids))
    attended = attended.reshape(frame_count, block_count, local_heads, HEAD_DIM, block_rows)
    attended = jnp.transpose(attended, (0, 2, 3, 1, 4)).reshape(frame_count, width, positions)
    update = add_mixed(lax.all_gather(attended, "heads", axis=1, tiled=True), spatial_out)
    after_spatial = (frame_tokens.astype(jnp.float32) + update).astype(jnp.bfloat16)
    own_rows = lax.all_to_all(after_spatial, "seq", split_axis=2, concat_axis=0, tiled=True)
    frames_all = own_rows.shape[0]
    columns = own_rows.shape[2]
    piece_add, piece_sq = project_piece(
        lax.all_gather(own_rows, "heads", axis=1, tiled=True),
        temporal_gain,
        temporal_qkv,
        slice(0, 3),
    )
    mixed_time = (piece_add * lax.rsqrt(piece_sq / D + epsilon)[:, None, None, :]).astype(
        jnp.bfloat16
    )
    mixed_time = mixed_time.reshape(frames_all, 3, local_heads, HEAD_DIM, columns)
    time_scores = jnp.einsum(
        "fhep,ghep->hfgp", mixed_time[:, 0], mixed_time[:, 1], preferred_element_type=jnp.float32
    )
    time_weights = softmax_along(time_scores * HEAD_DIM ** (-0.5), 2)
    attended_time = jnp.einsum(
        "hfgp,ghep->fhep", time_weights, mixed_time[:, 2], preferred_element_type=jnp.float32
    )
    attended_time = attended_time.astype(jnp.bfloat16).reshape(frames_all, width, columns)
    update_time = add_mixed(
        lax.all_gather(attended_time, "heads", axis=1, tiled=True), temporal_out
    )
    block_out = (own_rows.astype(jnp.float32) + update_time).astype(jnp.bfloat16)
    returned = lax.all_to_all(block_out, "seq", split_axis=0, concat_axis=2, tiled=True)
    half_width = width // 2
    partner = from_partner(returned, "cfg", 0)
    branch_index = lax.axis_index("cfg")
    cond_full = jnp.where(branch_index == 0, returned, partner)
    uncond_full = jnp.where(branch_index == 0, partner, returned)
    cond_part = lax.dynamic_slice_in_dim(cond_full, branch_index * half_width, half_width, 1)
    uncond_part = lax.dynamic_slice_in_dim(uncond_full, branch_index * half_width, half_width, 1)
    ratio = guide_numer.astype(jnp.float32) / guide_denom.astype(jnp.float32)
    cond_wide = cond_part.astype(jnp.float32)
    uncond_wide = uncond_part.astype(jnp.float32)
    return (uncond_wide + ratio[:, None, None] * (cond_wide - uncond_wide)).astype(jnp.bfloat16)


def solution(mesh):
    return jax.shard_map(
        shards,
        mesh=mesh,
        in_specs=(
            P("cfg", ("groups", "seq"), "heads", None),
            P("cfg", ("groups", "seq"), "heads", None),
            P("cfg", ("groups", "seq")),
            P(("groups", "seq")),
            P(("groups", "seq")),
            P(),
            P(None, "heads", None),
            P("heads", None),
            P(),
            P(None, "heads", None),
            P("heads", None),
        ),
        out_specs=P(("groups", "seq"), ("heads", "cfg"), None),
        check_vma=False,
    )
```

profile of v0, /device:TPU:0, one launch (start us, length us, event | category | flops | bytes accessed | tf_op | source)
XLA Modules:
  0.0 359.0 jit_solution(843548291912899709)
XLA Ops:
  6.5 0.0 copy-start
  6.5 0.0 all-gather.12.cloned.1.call-start
  6.5 0.7 all-gather.12.cloned.1.call-update
  7.3 0.0 all-gather.8.cloned.1.call-start
  7.3 0.7 convert_element_type.98
  8.7 7.7 %all-gather.1 = bf16[1,1,1152,128]{3,2,1,0:T(8,128)(2,1)S(1)} all-gather(bf16[1,1,576,128]{3,2,1,0:T(8,128)(2,1)} %param.14), channel_id=3, replica_groups=mesh['groups'=2,'seq'=4,'heads'=2,'cfg'=2] {'heads'}, dimensions={2}, use_global_device_ids=true | all-gather | bytes 442368 | tf_op jit(solution)/shard_map/all_gather | solution.py:55
  16.4 0.2 fusion.93
  16.6 3.0 fusion.87
  19.6 28.1 %all-gather.12.cloned.1.call-done = bf16[1,1,1152,1024]{3,2,1,0:T(8,128)(2,1)} async-done(((bf16[1,1,576,1024]{3,2,1,0:T(8,128)(2,1)}), bf16[1,1,1152,1024]{3,2,1,0:T(8,128)(2,1)}) %all-gather.12.cloned.1.call-update) | async-done | bytes 2359312 | tf_op jit(solution)/shard_map/all_gather | solution.py:54
  47.7 2.3 fusion.50
  50.0 0.0 copy-done.3
  50.1 7.3 %fusion.48 = bf16[1,1024,3,576]{1,3,2,0:T(8,128)(2,1)S(1)} fusion(f32[1024]{0:T(1024)S(1)} %add_rsqrt_fusion.1, bf16[3,576,1152]{2,1,0:T(8,128)(2,1)} %param.19, bf16[1,1,1152,1024]{3,2,1,0:T(8,128)(2,1)S(1)} %copy-done.3, f32[1152]{0:T(1024)S(1)} %convert_element_type.98), kind=kOutput, calls=%fused_computation.28 | convolution fusion | flops 4083941376 | bytes 9888256 | tf_op jit(solution)/shard_map/kod,fdp->fkop/dot_general | solution.py:26
  57.3 1.4 slice_bitcast_fusion
  58.7 1.3 pad_maximum_fusion
  60.1 37.0 %while.10 = (s32[]{:T(128)}, bf16[2,8,72,512]{3,2,1,0:T(8,128)(2,1)}, pred[1,1152]{1,0:T(4,128)(4,1)S(1)}, s32[2]{0:T(128)S(1)}, bf16[1,8,72,1024]{3,2,1,0:T(8,1...) while((s32[]{:T(128)}, ...), condition=%wide.region_5.6_spmd, body=%wide.region_2.5_spmd.sunk | while | flops 2081200384 | bytes 5788856 | solution.py:90
  60.5 0.7 dynamic_slice.50
  61.9 7.0 %exponential_reduce_fusion.2 = f32[8,512]{1,0:T(8,128)S(1)} fusion(pred[1152]{0:T(1024)(128)(4,1)S(1)} %reduce.5, bf16[1,8,72,1152]{3,2,1,0:T(8,128)(2,1)S(1)} %get-tuple-element.139, bf16[1,8,72,1024]{3,2,1,0:T(8,128)(2,1)} %get-tuple-element.138, s32[]{:T(128)S(6)} %select_n.52), kind=kOutput, calls=%fused_computation.5.clone.1 | convolution fusion | flops 698352768 | bytes 1934468 | tf_op jit(solution)/shard_map/while/body/eval_jaxpr/sub | solution.py:17
  69.0 9.8 %fusion.120 = bf16[2,8,72,512]{3,2,1,0:T(8,128)(2,1)} fusion(bf16[2,8,72,512]{3,2,1,0:T(8,128)(2,1)} %get-tuple-element.123, s32[]{:T(128)} %get-tuple-element.122, bf16[1,8,72,1152]{3,2,1,0:T(8,128)(2,1)} %get-tuple-element.140, f32[8,512]{1,0:T(8,128)S(1)} %exponential_reduce_fusion.2, pred[1152]{0:T(1024)(128)(4,1)S(1)} %reduce.5, ...), kind=kOutput, calls=%fused_computation.13.clone.1 | convolution fusion | flops 1382847616 | bytes 3851908 | tf_op jit(solution)/shard_map/while/body/eval_jaxpr/hpk,hek->hep/dot_general | solution.py:85
  78.8 0.7 dynamic_slice.50
  80.2 7.0 %exponential_reduce_fusion.2 = f32[8,512]{1,0:T(8,128)S(1)} fusion(pred[1152]{0:T(1024)(128)(4,1)S(1)} %reduce.5, bf16[1,8,72,1152]{3,2,1,0:T(8,128)(2,1)S(1)} %get-tuple-element.139, bf16[1,8,72,1024]{3,2,1,0:T(8,128)(2,1)} %get-tuple-element.138, s32[]{:T(128)S(6)} %select_n.52), kind=kOutput, calls=%fused_computation.5.clone.1 | convolution fusion | flops 698352768 | bytes 1934468 | tf_op jit(solution)/shard_map/while/body/eval_jaxpr/sub | solution.py:17
  87.2 9.8 %fusion.120 = bf16[2,8,72,512]{3,2,1,0:T(8,128)(2,1)} fusion(bf16[2,8,72,512]{3,2,1,0:T(8,128)(2,1)} %get-tuple-element.123, s32[]{:T(128)} %get-tuple-element.122, bf16[1,8,72,1152]{3,2,1,0:T(8,128)(2,1)} %get-tuple-element.140, f32[8,512]{1,0:T(8,128)S(1)} %exponential_reduce_fusion.2, pred[1152]{0:T(1024)(128)(4,1)S(1)} %reduce.5, ...), kind=kOutput, calls=%fused_computation.13.clone.1 | convolution fusion | flops 1382847616 | bytes 3851908 | tf_op jit(solution)/shard_map/while/body/eval_jaxpr/hpk,hek->hep/dot_general | solution.py:85
  97.1 2.5 copy.43
  99.6 1.7 reshape.105
  101.2 0.0 all-gather.8.cloned.1.call-update
  101.3 0.2 all-gather.14.cloned.1.call-start
  101.5 36.0 %all-gather.8.cloned.1.call-done = bf16[1,1152,1024]{2,1,0:T(8,128)(2,1)} async-done(((bf16[1,576,1024]{2,1,0:T(8,128)(2,1)}), bf16[1,1152,1024]{2,1,0:T(8,128)(2,1)}) %all-gather.8.cloned.1.call-update) | async-done | bytes 2359312 | tf_op jit(solution)/shard_map/all_gather | solution.py:93
  137.5 0.0 copy-done
  137.5 3.7 %fusion.64 = bf16[1,576,1024]{2,1,0:T(8,128)(2,1)S(1)} fusion(bf16[576,1152]{1,0:T(8,128)(2,1)S(1)} %copy-done, bf16[1,1152,1024]{2,1,0:T(8,128)(2,1)} %all-gather.8.cloned.1.call-done, bf16[1,1,576,1024]{3,2,1,0:T(8,128)(2,1)} %param.13), kind=kOutput, calls=%fused_computation.47 | convolution fusion | flops 1360723968 | bytes 6045696 | tf_op jit(solution)/shard_map/oc,fcp->fop/dot_general | solution.py:31
  141.1 4.1 %copy.44 = bf16[1,576,1024]{1,0,2:T(2,128)(2,1)} copy(bf16[1,576,1024]{2,1,0:T(8,128)(2,1)S(1)} %fusion.64) | data formatting | bytes 2359296 | tf_op jit(solution)/shard_map/convert_element_type | solution.py:94
  145.3 0.5 broadcast.82
  145.8 9.9 %reduce.3 = bf16[1024,576]{1,0:T(8,128)(2,1)S(1)} reduce(bf16[1024,1,576]{2,1,0:T(2,128)(2,1)} %bitcast.189, bf16[]{:T(256)} %broadcast.82), dimensions={1}, to_apply=%bitcast.164.reduce_sub_computation | reduce | bytes 2359298
  155.7 2.6 reshape.124
  158.3 33.0 %all_to_all.36 = bf16[4,2,73728]{2,1,0:T(2,128)(2,1)S(1)} all-to-all(bf16[4,2,73728]{2,1,0:T(2,128)(2,1)} %reshape.124), channel_id=1, replica_groups=mesh['groups'=2,'seq'=4,'heads'=2,'cfg'=2] {'seq'}, dimensions={0} | all-to-all | bytes 2359296 | tf_op jit(solution)/shard_map/all_to_all | solution.py:95
  191.3 3.3 reshape.125
  194.5 1.9 copy.57
  196.5 0.0 copy-start.5
  196.5 1.5 copy.46
  197.9 0.0 all-gather.14.cloned.1.call-update
  198.0 0.3 all-gather.10.cloned.1.call-start
  198.2 0.0 copy-done.5
  198.3 34.1 %all-gather.14.cloned.1.call-done = bf16[4,1,1152,256]{3,2,0,1:T(8,128)(2,1)} async-done(((bf16[4,1,576,256]{3,2,0,1:T(8,128)(2,1)}), bf16[4,1,1152,256]{3,2,0,1:T(8,128)(2,1)}) %all-gather.14.cloned.1.call-update) | async-done | bytes 2359312 | tf_op jit(solution)/shard_map/all_gather | solution.py:99
  232.3 2.3 fusion.52
  234.6 0.1 copy-done.4
  234.7 7.2 %multiply_convert_fusion = bf16[4,256,3,576]{1,3,2,0:T(8,128)(2,1)S(1)} fusion(f32[4,256]{1,0:T(4,128)S(1)} %add_rsqrt_fusion, bf16[3,576,1152]{2,1,0:T(8,128)(2,1)} %param.22, bf16[4,1,1152,256]{3,2,0,1:T(8,128)(2,1)S(1)} %copy-done.4, f32[1152]{0:T(1024)S(1)} %convert_element_type.109), kind=kOutput, calls=%fused_computation.29 | convolution fusion | flops 4083941376 | bytes 9888256 | tf_op jit(solution)/shard_map/kod,fdp->fkop/dot_general | solution.py:26
  241.9 1.9 fusion.104
  243.8 2.8 copy.59
  246.7 4.1 %copy.60 = bf16[4,1,8,72,256]{3,0,4,2,1:T(4,128)(2,1)} copy(bf16[4,1,8,72,256]{4,3,2,1,0:T(8,128)(2,1)} %get-tuple-element.59) | data formatting | bytes 2359296
  250.7 5.8 %fusion.71 = f32[8,256,4,4]{3,2,1,0:T(4,128)} fusion(bf16[4,1,8,72,256]{3,0,4,2,1:T(4,128)(2,1)} %copy.60, bf16[4,1,8,72,256]{3,0,4,2,1:T(4,128)(2,1)S(1)} %copy.59), kind=kOutput, calls=%fused_computation.54 | convolution fusion | flops 4718592 | bytes 2490368 | tf_op jit(solution)/shard_map/fhep,ghep->hfgp/dot_general | solution.py:108
  256.5 2.8 copy.50
  259.4 0.0 copy-start.1
  259.5 2.1 copy.51
  261.6 0.0 copy-done.1
  261.6 2.5 copy.58
  264.1 5.8 %convert_bitcast_fusion = bf16[4,8,72,256]{2,0,3,1:T(4,128)(2,1)} fusion(bf16[8,4,4,256]{2,1,3,0:T(4,128)(2,1)} %copy.51, bf16[4,1,8,72,256]{3,0,4,2,1:T(4,128)(2,1)} %copy.58), kind=kOutput, calls=%fused_computation.59 | convolution fusion | flops 5308416 | bytes 2424832 | tf_op jit(solution)/shard_map/hfgp,ghep->fhep/dot_general | solution.py:112
  269.9 4.2 %copy.52 = bf16[4,8,72,256]{3,2,1,0:T(8,128)(2,1)} copy(bf16[4,8,72,256]{2,0,3,1:T(4,128)(2,1)} %convert_bitcast_fusion) | data formatting | bytes 2359296 | tf_op jit(solution)/shard_map/convert_element_type | solution.py:115
  274.1 0.0 all-gather.10.cloned.1.call-update
  274.1 36.2 %all-gather.10.cloned.1.call-done = bf16[4,1152,256]{2,1,0:T(8,128)(2,1)} async-done(((bf16[4,576,256]{2,1,0:T(8,128)(2,1)}), bf16[4,1152,256]{2,1,0:T(8,128)(2,1)}) %all-gather.10.cloned.1.call-update) | async-done | bytes 2359312 | tf_op jit(solution)/shard_map/all_gather | solution.py:117
  310.3 0.0 copy-done.2
  310.3 3.8 %fusion.63 = bf16[4,576,256]{2,1,0:T(8,128)(2,1)S(1)} fusion(bf16[4,1152,256]{2,1,0:T(8,128)(2,1)} %all-gather.10.cloned.1.call-done, bf16[576,1152]{1,0:T(8,128)(2,1)} %param.23, bf16[1,576,4,256]{3,1,2,0:T(8,128)(2,1)S(1)} %copy-done.2), kind=kOutput, calls=%fused_computation.45 | convolution fusion | flops 1360723968 | bytes 6045696 | tf_op jit(solution)/shard_map/oc,fcp->fop/dot_general | solution.py:31
  314.1 32.8 %all_to_all.37 = bf16[4,576,256]{2,1,0:T(8,128)(2,1)S(1)} all-to-all(bf16[4,576,256]{2,1,0:T(8,128)(2,1)S(1)} %fusion.63), channel_id=1, replica_groups=mesh['groups'=2,'seq'=4,'heads'=2,'cfg'=2] {'seq'}, dimensions={0} | all-to-all | bytes 2359296 | tf_op jit(solution)/shard_map/all_to_all | solution.py:120
  346.8 0.1 copy.61
  347.0 0.1 collective-permute-start
  348.4 1.6 collective-permute-done
  350.0 2.2 fusion.91
  (17 shorter events, 0.2 us)
Async XLA Ops:
  6.5 130.9 %copy-start = (bf16[576,1152]{1,0:T(8,128)(2,1)S(1)}, bf16[576,1152]{1,0:T(8,128)(2,1)}, u32[]{:S(2)}) copy-start(bf16[576,1152]{1,0:T(8,128)(2,1)} %param.20) | copy-start | bytes 3981316
  6.5 41.1 %all-gather.12.cloned.1.call-start = ((), (), s32[]{:S(2)}) async-start(), calls=%async_computation.4 | async-start | bytes 3538944 | tf_op jit(solution)/shard_map/all_gather | solution.py:54
  7.3 130.2 %all-gather.8.cloned.1.call-start = ((), (), s32[]{:S(2)}) async-start(), calls=%async_computation.2 | async-start | bytes 3538944 | tf_op jit(solution)/shard_map/all_gather | solution.py:93
  47.7 2.4 copy-start.3
  101.3 131.0 %all-gather.14.cloned.1.call-start = ((), (), s32[]{:S(2)}) async-start(), calls=%async_computation.5 | async-start | bytes 3538944 | tf_op jit(solution)/shard_map/all_gather | solution.py:99
  196.5 1.8 copy-start.5
  198.0 112.3 %all-gather.10.cloned.1.call-start = ((), (), s32[]{:S(2)}) async-start(), calls=%async_computation.3 | async-start | bytes 3538944 | tf_op jit(solution)/shard_map/all_gather | solution.py:117
  232.3 2.4 copy-start.4
  259.4 2.2 copy-start.1
  269.9 40.4 %copy-start.2 = (bf16[1,576,4,256]{3,1,2,0:T(8,128)(2,1)S(1)}, bf16[1,576,4,256]{3,1,2,0:T(8,128)(2,1)}, u32[]{:S(2)}) copy-start(bf16[1,576,4,256]{3,1,2,0:T(8,128)(2,1)} %copy.46) | copy-start | bytes 3538948
  347.0 3.0 collective-permute-start
Sparse Core Ops, SparseCore 0:
  8.9 38.7 all-gather.11
  101.4 36.0 all-gather.7
  198.1 34.1 all-gather.13
  274.2 36.0 all-gather.9
where the time goes:
time: 364 us; the launch traced here: 359 us
  waiting for transfers between devices  137 us (38%)
  blocking collectives  73.5 us (20%)
  matrix products  70.3 us (19%)
  local copies, waits for them, and re-layouts  41.4 us (11%)
  other arithmetic  19.1 us (5%)
  between operations  15.5 us (4%)
    all_gather x1, waiting for transfers between devices, shards(): lax.all_gather(attended_time, 'heads', axis=1, tiled=True)  36.2 us
    all_gather x1, waiting for transfers between devices, shards(): lax.all_gather(attended, 'heads', axis=1, tiled=True)  36 us
    all_gather x1, waiting for transfers between devices, shards(): lax.all_gather(own_rows, 'heads', axis=1, tiled=True)  34.1 us
    all_to_all x1, blocking collectives, shards(): lax.all_to_all(after_spatial, 'seq', split_axis=2, concat_axis=0, tiled=T...  33 us
    all_to_all x1, blocking collectives, shards(): lax.all_to_all(block_out, 'seq', split_axis=0, concat_axis=2, tiled=True)  32.8 us
    all_gather x1, waiting for transfers between devices, shards(): video_piece = lax.all_gather(frame_tokens, 'heads', axis=1, tiled=True)  28.1 us
    dot_general x2, matrix products, block_step(): jnp.einsum('hpk,hek->hep', weights, value_rows[frame_id], preferred_eleme...  19.7 us
    unnamed x19, local copies, waits for them, and re-layouts  17.8 us
  transfers between devices with their start and end apart: 5, of which 5 were waited for; matrix products, arithmetic and copies ran while one was open for 1% of the time, Pallas kernels for 0%

commit v1 on v0

--- a/solution.py
+++ b/solution.py
@@ -2,6 +2,7 @@
 import jax.numpy as jnp
 from jax import lax
 from jax.sharding import PartitionSpec as P
+from jax.lax import axis_index, axis_size, ppermute
 
 D = 1152
 HEAD_DIM = 72
@@ -92,7 +93,24 @@
     attended = jnp.transpose(attended, (0, 2, 3, 1, 4)).reshape(frame_count, width, positions)
     update = add_mixed(lax.all_gather(attended, "heads", axis=1, tiled=True), spatial_out)
     after_spatial = (frame_tokens.astype(jnp.float32) + update).astype(jnp.bfloat16)
-    own_rows = lax.all_to_all(after_spatial, "seq", split_axis=2, concat_axis=0, tiled=True)
+    work_now = axis_size("seq")
+    formed = axis_index("seq")
+    frame_out, f_now = (work_now, formed)
+    kept_arr = list(after_spatial.shape)
+    res = after_spatial.shape[2] // frame_out
+    kept_arr[2] = res
+    local_next = kept_arr[0]
+    kept_arr[0] = local_next * frame_out
+    tick = 0
+    own_rows = jnp.zeros(kept_arr, after_spatial.dtype)
+    while tick < frame_out:
+        y1 = lax.dynamic_slice_in_dim(after_spatial, (f_now ^ tick) * res, res, axis=2)
+        if tick:
+            y1 = ppermute(y1, "seq", tuple(((dev_i, dev_i ^ tick) for dev_i in range(frame_out))))
+        own_rows = lax.dynamic_update_slice_in_dim(
+            own_rows, y1, (f_now ^ tick) * local_next, axis=0
+        )
+        tick += 1
     frames_all = own_rows.shape[0]
     columns = own_rows.shape[2]
     piece_add, piece_sq = project_piece(

time: 364 us -> 334 us (0.918); the launches traced: 359 us -> 333 us
  blocking collectives: 73.5 us -> 40.5 us
  waiting for transfers between devices: 137 us -> 160 us
  other arithmetic: 19.1 us -> 9.16 us
  local copies, waits for them, and re-layouts: 41.4 us -> 31.7 us
  starting transfers between devices: 0.58 us -> 4.87 us
    all_to_all x1 -> x0, blocking collectives: 33 us -> none  [shards(): lax.all_to_all(after_spatial, 'seq', split_axis=2, concat_axis=0, tiled=T...]
    ppermute x0 -> x3, waiting for transfers between devices: none -> 19.6 us  [shards(): ppermute(y1, 'seq', tuple(((dev_i, dev_i ^ tick) for dev_i in range(frame...]
    unnamed x1 -> x0, other arithmetic: 9.93 us -> none
    unnamed x19 -> x17, local copies, waits for them, and re-layouts: 17.8 us -> 10.5 us
    ppermute x0 -> x3, starting transfers between devices: none -> 4.45 us  [shards(): ppermute(y1, 'seq', tuple(((dev_i, dev_i ^ tick) for dev_i in range(frame...]
    convert_element_type x1 -> x0, local copies, waits for them, and re-layouts: 4.11 us -> none  [shards(): (frame_tokens.astype(jnp.float32) + update).astype(jnp.bfloat16)]
    all_gather x1, waiting for transfers between devices: 34.1 us -> 38.1 us  [shards(): lax.all_gather(own_rows, 'heads', axis=1, tiled=True)]
  transfers between devices with their start and end apart: 5 -> 8, of which waited for: 5 -> 7; matrix products, arithmetic and copies ran while one was open for 1% -> 2% of each run, Pallas kernels for 0% -> 0%
where the time goes in v1:
time: 334 us; the launch traced here: 333 us
  waiting for transfers between devices  160 us (48%)
  matrix products  70.3 us (21%)
  blocking collectives  40.5 us (12%)
  local copies, waits for them, and re-layouts  31.7 us (9%)
  between operations  15.4 us (5%)
  other arithmetic  9.16 us (3%)
  starting transfers between devices  4.87 us (1%)
    all_gather x1, waiting for transfers between devices, shards(): lax.all_gather(own_rows, 'heads', axis=1, tiled=True)  38.1 us
    all_gather x1, waiting for transfers between devices, shards(): lax.all_gather(attended_time, 'heads', axis=1, tiled=True)  36.2 us
    all_gather x1, waiting for transfers between devices, shards(): lax.all_gather(attended, 'heads', axis=1, tiled=True)  35.9 us
    all_to_all x1, blocking collectives, shards(): lax.all_to_all(block_out, 'seq', split_axis=0, concat_axis=2, tiled=True)  32.8 us
    all_gather x1, waiting for transfers between devices, shards(): video_piece = lax.all_gather(frame_tokens, 'heads', axis=1, tiled=True)  28.1 us
    dot_general x2, matrix products, block_step(): jnp.einsum('hpk,hek->hep', weights, value_rows[frame_id], preferred_eleme...  19.7 us
    ppermute x3, waiting for transfers between devices, shards(): ppermute(y1, 'seq', tuple(((dev_i, dev_i ^ tick) for dev_i in range(frame...  19.6 us
    dot_general x3, matrix products, project_piece(): jnp.einsum('kod,fdp->fkop', weight_piece, scaled, preferred_element_type=...  17.5 us
  transfers between devices with their start and end apart: 8, of which 7 were waited for; matrix products, arithmetic and copies ran while one was open for 2% of the time, Pallas kernels for 0%

profile of v1, /device:TPU:0, one launch (start us, length us, event | category | flops | bytes accessed | tf_op | source)
XLA Modules:
  0.0 333.5 jit_solution(6464101008968819925)
XLA Ops:
  6.5 0.0 copy-start
  6.5 0.0 all-gather.13.cloned.1.call-start
  6.5 0.7 all-gather.13.cloned.1.call-update
  7.3 0.0 all-gather.7.cloned.1.call-start
  7.3 0.7 convert_element_type.98
  8.7 7.7 %all-gather.1 = bf16[1,1,1152,128]{3,2,1,0:T(8,128)(2,1)S(1)} all-gather(bf16[1,1,576,128]{3,2,1,0:T(8,128)(2,1)} %param.14), channel_id=3, replica_groups=mesh['groups'=2,'seq'=4,'heads'=2,'cfg'=2] {'heads'}, dimensions={2}, use_global_device_ids=true | all-gather | bytes 442368 | tf_op jit(solution)/shard_map/all_gather | solution.py:56
  16.4 0.2 fusion.92
  16.6 3.0 fusion.86
  19.6 28.1 %all-gather.13.cloned.1.call-done = bf16[1,1,1152,1024]{3,2,1,0:T(8,128)(2,1)} async-done(((bf16[1,1,576,1024]{3,2,1,0:T(8,128)(2,1)}), bf16[1,1,1152,1024]{3,2,1,0:T(8,128)(2,1)}) %all-gather.13.cloned.1.call-update) | async-done | bytes 2359312 | tf_op jit(solution)/shard_map/all_gather | solution.py:55
  47.7 2.3 fusion.52
  50.0 0.0 copy-done.4
  50.1 7.3 %fusion.48 = bf16[1,1024,3,576]{1,3,2,0:T(8,128)(2,1)S(1)} fusion(f32[1024]{0:T(1024)S(1)} %add_rsqrt_fusion.1, bf16[3,576,1152]{2,1,0:T(8,128)(2,1)} %param.19, bf16[1,1,1152,1024]{3,2,1,0:T(8,128)(2,1)S(1)} %copy-done.4, f32[1152]{0:T(1024)S(1)} %convert_element_type.98), kind=kOutput, calls=%fused_computation.28 | convolution fusion | flops 4083941376 | bytes 9888256 | tf_op jit(solution)/shard_map/kod,fdp->fkop/dot_general | solution.py:27
  57.3 1.4 slice_bitcast_fusion
  58.7 1.3 pad_maximum_fusion
  60.0 36.4 %while.10 = (s32[]{:T(128)}, bf16[2,8,72,512]{3,2,1,0:T(8,128)(2,1)}, pred[1,1152]{1,0:T(4,128)(4,1)S(1)}, s32[2]{0:T(128)S(1)}, bf16[1,8,72,1024]{3,2,1,0:T(8,1...) while((s32[]{:T(128)}, ...), condition=%wide.region_5.6_spmd, body=%wide.region_2.5_spmd.sunk | while | flops 2081200384 | bytes 5788856 | solution.py:91
  60.0 0.6 dynamic_slice.70
  61.4 7.0 %exponential_reduce_fusion.2 = f32[8,512]{1,0:T(8,128)S(1)} fusion(pred[1152]{0:T(1024)(128)(4,1)S(1)} %reduce.4, bf16[1,8,72,1152]{3,2,1,0:T(8,128)(2,1)S(1)} %get-tuple-element.143, bf16[1,8,72,1024]{3,2,1,0:T(8,128)(2,1)} %get-tuple-element.142, s32[]{:T(128)S(6)} %select_n.84), kind=kOutput, calls=%fused_computation.5.clone.1 | convolution fusion | flops 698352768 | bytes 1934468 | tf_op jit(solution)/shard_map/while/body/eval_jaxpr/sub | solution.py:18
  68.4 9.9 %fusion.119 = bf16[2,8,72,512]{3,2,1,0:T(8,128)(2,1)} fusion(bf16[2,8,72,512]{3,2,1,0:T(8,128)(2,1)} %get-tuple-element.127, s32[]{:T(128)} %get-tuple-element.126, bf16[1,8,72,1152]{3,2,1,0:T(8,128)(2,1)} %get-tuple-element.144, f32[8,512]{1,0:T(8,128)S(1)} %exponential_reduce_fusion.2, pred[1152]{0:T(1024)(128)(4,1)S(1)} %reduce.4, ...), kind=kOutput, calls=%fused_computation.13.clone.1 | convolution fusion | flops 1382847616 | bytes 3851908 | tf_op jit(solution)/shard_map/while/body/eval_jaxpr/hpk,hek->hep/dot_general | solution.py:86
  78.2 0.6 dynamic_slice.70
  79.6 7.0 %exponential_reduce_fusion.2 = f32[8,512]{1,0:T(8,128)S(1)} fusion(pred[1152]{0:T(1024)(128)(4,1)S(1)} %reduce.4, bf16[1,8,72,1152]{3,2,1,0:T(8,128)(2,1)S(1)} %get-tuple-element.143, bf16[1,8,72,1024]{3,2,1,0:T(8,128)(2,1)} %get-tuple-element.142, s32[]{:T(128)S(6)} %select_n.84), kind=kOutput, calls=%fused_computation.5.clone.1 | convolution fusion | flops 698352768 | bytes 1934468 | tf_op jit(solution)/shard_map/while/body/eval_jaxpr/sub | solution.py:18
  86.6 9.8 %fusion.119 = bf16[2,8,72,512]{3,2,1,0:T(8,128)(2,1)} fusion(bf16[2,8,72,512]{3,2,1,0:T(8,128)(2,1)} %get-tuple-element.127, s32[]{:T(128)} %get-tuple-element.126, bf16[1,8,72,1152]{3,2,1,0:T(8,128)(2,1)} %get-tuple-element.144, f32[8,512]{1,0:T(8,128)S(1)} %exponential_reduce_fusion.2, pred[1152]{0:T(1024)(128)(4,1)S(1)} %reduce.4, ...), kind=kOutput, calls=%fused_computation.13.clone.1 | convolution fusion | flops 1382847616 | bytes 3851908 | tf_op jit(solution)/shard_map/while/body/eval_jaxpr/hpk,hek->hep/dot_general | solution.py:86
  96.4 2.5 copy.23
  98.9 1.7 reshape.105
  100.6 0.0 all-gather.7.cloned.1.call-update
  100.6 0.3 all-gather.9.cloned.1.call-start
  100.9 35.9 %all-gather.7.cloned.1.call-done = bf16[1,1152,1024]{2,1,0:T(8,128)(2,1)} async-done(((bf16[1,576,1024]{2,1,0:T(8,128)(2,1)}), bf16[1,1152,1024]{2,1,0:T(8,128)(2,1)}) %all-gather.7.cloned.1.call-update) | async-done | bytes 2359312 | tf_op jit(solution)/shard_map/all_gather | solution.py:94
  136.8 3.7 %fusion.63 = bf16[1,576,1024]{2,1,0:T(8,128)(2,1)S(1)} fusion(bf16[576,1152]{1,0:T(8,128)(2,1)S(1)} %copy-done, bf16[1,1152,1024]{2,1,0:T(8,128)(2,1)} %all-gather.7.cloned.1.call-done, bf16[1,1,576,1024]{3,2,1,0:T(8,128)(2,1)} %param.13), kind=kOutput, calls=%fused_computation.45 | convolution fusion | flops 1360723968 | bytes 6045696 | tf_op jit(solution)/shard_map/oc,fcp->fop/dot_general | solution.py:32
  140.5 0.1 broadcast_in_dim.24
  140.6 0.0 copy-start.6
  140.6 0.2 constant_dynamic-slice_fusion
  140.8 1.6 collective-permute-start
  142.3 2.4 collective-permute-start.1
  144.7 0.5 collective-permute-start.2
  145.2 9.8 %collective-permute-done = bf16[1,576,256]{2,1,0:T(8,128)(2,1)} collective-permute-done((bf16[1,576,256]{2,1,0:T(8,128)(2,1)S(1)}, bf16[1,576,256]{2,1,0:T(8,128)(2,1)}, u32[]{:S(2)}, u32[]{:S(2)}) %collective-permute-start) | collective-permute-done | bytes 294944 | tf_op jit(solution)/shard_map/ppermute | solution.py:109
  155.0 1.0 constant_dynamic-update-slice_fusion.2
  155.9 9.9 %collective-permute-done.1 = bf16[1,576,256]{2,1,0:T(8,128)(2,1)} collective-permute-done((bf16[1,576,256]{2,1,0:T(8,128)(2,1)S(1)}, bf16[1,576,256]{2,1,0:T(8,128)(2,1)}, u32[]{:S(2)}, u32[]{:S(2)}) %collective-permute-start.1) | collective-permute-done | bytes 294944 | tf_op jit(solution)/shard_map/ppermute | solution.py:109
  165.8 1.0 constant_dynamic-update-slice_fusion.1
  166.8 0.0 collective-permute-done.2
  166.8 1.0 constant_dynamic-update-slice_fusion
  167.8 1.0 copy-done.2
  168.9 0.0 all-gather.9.cloned.1.call-update
  168.9 0.0 all-gather.11.cloned.1.call-start
  168.9 0.0 copy-done.6
  169.0 38.1 %all-gather.9.cloned.1.call-done = bf16[4,1152,256]{2,1,0:T(8,128)(2,1)} async-done(((bf16[4,576,256]{2,1,0:T(8,128)(2,1)}), bf16[4,1152,256]{2,1,0:T(8,128)(2,1)}) %all-gather.9.cloned.1.call-update) | async-done | bytes 2359312 | tf_op jit(solution)/shard_map/all_gather | solution.py:117
  207.0 2.3 fusion.50
  209.3 0.1 copy-done.5
  209.4 7.2 %multiply_convert_fusion = bf16[4,256,3,576]{1,3,2,0:T(8,128)(2,1)S(1)} fusion(f32[4,256]{1,0:T(4,128)S(1)} %add_rsqrt_fusion, bf16[3,576,1152]{2,1,0:T(8,128)(2,1)} %param.22, bf16[4,1152,256]{2,1,0:T(8,128)(2,1)S(1)} %copy-done.5, f32[1152]{0:T(1024)S(1)} %convert_element_type.109), kind=kOutput, calls=%fused_computation.29 | convolution fusion | flops 4083941376 | bytes 9888256 | tf_op jit(solution)/shard_map/kod,fdp->fkop/dot_general | solution.py:27
  216.7 1.9 fusion.103
  218.5 2.8 copy.33
  221.4 4.0 %copy.34 = bf16[4,1,8,72,256]{3,0,4,2,1:T(4,128)(2,1)} copy(bf16[4,1,8,72,256]{4,3,2,1,0:T(8,128)(2,1)} %get-tuple-element.59) | data formatting | bytes 2359296
  225.4 5.8 %fusion.70 = f32[8,256,4,4]{3,2,1,0:T(4,128)} fusion(bf16[4,1,8,72,256]{3,0,4,2,1:T(4,128)(2,1)} %copy.34, bf16[4,1,8,72,256]{3,0,4,2,1:T(4,128)(2,1)S(1)} %copy.33), kind=kOutput, calls=%fused_computation.53 | convolution fusion | flops 4718592 | bytes 2490368 | tf_op jit(solution)/shard_map/fhep,ghep->hfgp/dot_general | solution.py:126
  231.3 2.8 copy.27
  234.2 2.0 copy.28
  236.3 2.5 copy.32
  238.7 5.8 %convert_bitcast_fusion = bf16[4,8,72,256]{2,0,3,1:T(4,128)(2,1)} fusion(bf16[8,4,4,256]{2,1,3,0:T(4,128)(2,1)} %copy.28, bf16[4,1,8,72,256]{3,0,4,2,1:T(4,128)(2,1)} %copy.32), kind=kOutput, calls=%fused_computation.58 | convolution fusion | flops 5308416 | bytes 2424832 | tf_op jit(solution)/shard_map/hfgp,ghep->fhep/dot_general | solution.py:130
  244.6 4.2 %copy.29 = bf16[4,8,72,256]{3,2,1,0:T(8,128)(2,1)} copy(bf16[4,8,72,256]{2,0,3,1:T(4,128)(2,1)} %convert_bitcast_fusion) | data formatting | bytes 2359296 | tf_op jit(solution)/shard_map/convert_element_type | solution.py:133
  248.8 0.0 all-gather.11.cloned.1.call-update
  248.8 36.2 %all-gather.11.cloned.1.call-done = bf16[4,1152,256]{2,1,0:T(8,128)(2,1)} async-done(((bf16[4,576,256]{2,1,0:T(8,128)(2,1)}), bf16[4,1152,256]{2,1,0:T(8,128)(2,1)}) %all-gather.11.cloned.1.call-update) | async-done | bytes 2359312 | tf_op jit(solution)/shard_map/all_gather | solution.py:135
  285.0 3.8 %fusion.64 = bf16[4,576,256]{2,1,0:T(8,128)(2,1)S(1)} fusion(bf16[4,576,256]{2,1,0:T(8,128)(2,1)S(1)} %copy-done.3, bf16[4,1152,256]{2,1,0:T(8,128)(2,1)} %all-gather.11.cloned.1.call-done, bf16[576,1152]{1,0:T(8,128)(2,1)} %param.23), kind=kOutput, calls=%fused_computation.47 | convolution fusion | flops 1360723968 | bytes 6045696 | tf_op jit(solution)/shard_map/oc,fcp->fop/dot_general | solution.py:32
  288.8 32.8 %all_to_all.18 = bf16[4,576,256]{2,1,0:T(8,128)(2,1)S(1)} all-to-all(bf16[4,576,256]{2,1,0:T(8,128)(2,1)S(1)} %fusion.64), channel_id=1, replica_groups=mesh['groups'=2,'seq'=4,'heads'=2,'cfg'=2] {'seq'}, dimensions={0} | all-to-all | bytes 2359296 | tf_op jit(solution)/shard_map/all_to_all | solution.py:138
  321.6 0.1 copy.35
  321.7 0.1 collective-permute-start.3
  323.1 1.6 collective-permute-done.3
  324.8 2.2 fusion.90
  (22 shorter events, 0.2 us)
Async XLA Ops:
  6.5 130.3 %copy-start = (bf16[576,1152]{1,0:T(8,128)(2,1)S(1)}, bf16[576,1152]{1,0:T(8,128)(2,1)}, u32[]{:S(2)}) copy-start(bf16[576,1152]{1,0:T(8,128)(2,1)} %param.20) | copy-start | bytes 3981316
  6.5 41.1 %all-gather.13.cloned.1.call-start = ((), (), s32[]{:S(2)}) async-start(), calls=%async_computation.4 | async-start | bytes 3538944 | tf_op jit(solution)/shard_map/all_gather | solution.py:55
  7.3 129.5 %all-gather.7.cloned.1.call-start = ((), (), s32[]{:S(2)}) async-start(), calls=%async_computation.1 | async-start | bytes 3538944 | tf_op jit(solution)/shard_map/all_gather | solution.py:94
  47.7 2.4 copy-start.4
  100.6 106.4 %all-gather.9.cloned.1.call-start = ((), (), s32[]{:S(2)}) async-start(), calls=%async_computation.2 | async-start | bytes 3538944 | tf_op jit(solution)/shard_map/all_gather | solution.py:117
  140.6 28.4 %copy-start.6 = (bf16[1152]{0:T(1024)(128)(2,1)S(1)}, bf16[1152]{0:T(1024)(128)(2,1)}, u32[]{:S(2)}) copy-start(bf16[1152]{0:T(1024)(128)(2,1)} %param.21) | copy-start | bytes 6916
  140.8 14.2 %collective-permute-start = (bf16[1,576,256]{2,1,0:T(8,128)(2,1)S(1)}, bf16[1,576,256]{2,1,0:T(8,128)(2,1)}, u32[]{:S(2)}, u32[]{:S(2)}) collective-permute-start(bf16[1,576,256]{2,1,0:T(8,128)(2,1)S(1)} %get-tuple-element.65), channel_id=1, source_target_pairs={{0,4},{4,0},{8,12},{12,8},{1,5},{5,1},{9,13},{13,9},{2,6},{6,2},{1... | collective-permute-start | bytes 884744 | tf_op jit(solution)/shard_map/ppermute | solution.py:109
  142.3 23.5 %collective-permute-start.1 = (bf16[1,576,256]{2,1,0:T(8,128)(2,1)S(1)}, bf16[1,576,256]{2,1,0:T(8,128)(2,1)}, u32[]{:S(2)}, u32[]{:S(2)}) collective-permute-start(bf16[1,576,256]{2,1,0:T(8,128)(2,1)S(1)} %get-tuple-element.64), channel_id=1, source_target_pairs={{0,8},{4,12},{8,0},{12,4},{1,9},{5,13},{9,1},{13,5},{2,10},{6,14},... | collective-permute-start | bytes 884744 | tf_op jit(solution)/shard_map/ppermute | solution.py:109
  144.7 22.1 %collective-permute-start.2 = (bf16[1,576,256]{2,1,0:T(8,128)(2,1)S(1)}, bf16[1,576,256]{2,1,0:T(8,128)(2,1)}, u32[]{:S(2)}, u32[]{:S(2)}) collective-permute-start(bf16[1,576,256]{2,1,0:T(8,128)(2,1)S(1)} %get-tuple-element.63), channel_id=1, source_target_pairs={{0,12},{4,8},{8,4},{12,0},{1,13},{5,9},{9,5},{13,1},{2,14},{6,10},... | collective-permute-start | bytes 884744 | tf_op jit(solution)/shard_map/ppermute | solution.py:109
  167.8 1.0 copy-start.2
  168.9 116.1 %all-gather.11.cloned.1.call-start = ((), (), s32[]{:S(2)}) async-start(), calls=%async_computation.3 | async-start | bytes 3538944 | tf_op jit(solution)/shard_map/all_gather | solution.py:135
  207.0 2.4 copy-start.5
  234.1 2.1 copy-start.1
  244.6 40.4 %copy-start.3 = (bf16[4,576,256]{2,1,0:T(8,128)(2,1)S(1)}, bf16[4,576,256]{2,1,0:T(8,128)(2,1)}, u32[]{:S(2)}) copy-start(bf16[4,576,256]{2,1,0:T(8,128)(2,1)} %copy-done.2) | copy-start | bytes 3538948
  321.7 3.0 collective-permute-start.3
Sparse Core Ops, SparseCore 0:
  8.9 38.7 all-gather.12
  100.7 36.0 all-gather.6
  169.0 37.9 all-gather.8
  248.9 36.0 all-gather.10
